TPU v7x, 32 devices: a whole 2x2x4 slice. The times are simulated.
32 devices in a mesh: grp: 2 (over y), exp: 4 (over z), tp: 4 (over x, core).
Axes of the slice: x: 2, y: 2, z: 4, core: 2. Of those that a mesh axis runs over, the one named last changes fastest.
Arguments:
- tokens: bfloat16 [128, 3584], P(('grp', 'exp'), 'tp'), parts along dimension 0, may hold values from -6 to 6
- gate_up_weight: bfloat16 [3584, 2, 18944], P('tp', None, 'exp'), may hold values from -0.09375 to 0.09375
- down_weight: bfloat16 [18944, 3584], P('exp', 'tp'), may hold values from -0.046875 to 0.046875
- adapter_in: bfloat16 [4, 3584, 16], P('exp', 'tp'), may hold values from -0.09375 to 0.09375
- adapter_out: bfloat16 [4, 16, 3584], P('exp', None, 'tp'), may hold values from -1.5 to 1.5
- expert_ids: int32 [128, 2], P(('grp', 'exp')), parts along dimension 0, may hold values from 0 to 3, all different within a row; in each aligned block of 16 rows (0 to 15, 16 to 31, ...) at most 16 rows name the same one
- route_weight: float32 [128, 2], P(('grp', 'exp')), parts along dimension 0, may hold values from 0.2 to 1
Outputs:
- mixed: bfloat16 [128, 3584], P(('grp', 'exp'), 'tp'), parts along dimension 0
There are 2 independent parts, one for each index of `grp`. A program takes and returns all parts, laid end to end along the dimension named above; an argument that names none is the same for every part. Nothing has to cross between parts.
Inputs may be any that keep to these rules, and one draw needn't show every extreme that they name: `expert_ids`: each row names 2 different experts. Among the 16 rows of one index of exp (aligned blocks of 16 rows) no expert is named by more than 16 rows, and in every draw some expert is named by exactly 16 rows of some block.
All inputs are finite; a program needn't handle non-finite values.
Results may differ from a plain program's by a relative error of at most 0.025.
Values may be sent and summed in bfloat16 or wider, within the bound.
No kernel may reach another device: no remote copies, remote signals or barrier semaphores. Data moves between devices by JAX's collectives and lax.ppermute only.
A program may use at most 64 MiB of HBM per device.

v0:
```python
import jax
import jax.numpy as jnp
from jax import lax
from jax.sharding import PartitionSpec as P


def local(tokens, gate_up_weight, down_weight, adapter_in, adapter_out, expert_ids, route_weight):
    exp_count = lax.axis_size("exp")
    own_rows, feat_width = tokens.shape
    all_tokens = lax.all_gather(tokens, "exp", axis=0, tiled=True)
    hidden_width = gate_up_weight.shape[2]
    pair_weight = gate_up_weight.reshape(feat_width, 2 * hidden_width)
    pair_share = lax.psum_scatter(
        jnp.dot(all_tokens, pair_weight, preferred_element_type=jnp.float32).astype(jnp.bfloat16),
        "tp",
        scatter_dimension=0,
        tiled=True,
    ).astype(jnp.float32)
    hidden_share = (
        jax.nn.silu(pair_share[:, :hidden_width]) * pair_share[:, hidden_width:]
    ).astype(jnp.bfloat16)
    hidden = lax.all_gather(hidden_share, "tp", axis=0, tiled=True)
    base_out = lax.psum_scatter(
        jnp.dot(hidden, down_weight, preferred_element_type=jnp.float32).astype(jnp.bfloat16),
        "exp",
        scatter_dimension=0,
        tiled=True,
    ).astype(jnp.float32)
    top_count = expert_ids.shape[1]
    expert_count = adapter_in.shape[0] * exp_count
    flat_ids = expert_ids.reshape(own_rows * top_count)
    flat_weight = route_weight.reshape(own_rows * top_count)
    expert_hits = (flat_ids[:, None] == jnp.arange(expert_count, dtype=jnp.int32)[None, :]).astype(
        jnp.int32
    )
    capacity = max(2, 2 * top_count * own_rows // expert_count)
    slot_index = jnp.sum((jnp.cumsum(expert_hits, axis=0) - expert_hits) * expert_hits, axis=1)
    slot_target = flat_ids * capacity + slot_index
    slot_hits = (
        slot_target[:, None] == jnp.arange(expert_count * capacity, dtype=jnp.int32)[None, :]
    )
    combine_matrix = jnp.sum(
        (slot_hits.astype(jnp.float32) * flat_weight[:, None]).reshape(
            own_rows, top_count, expert_count * capacity
        ),
        axis=1,
    )
    dispatch_matrix = slot_hits.T.astype(jnp.bfloat16)
    repeated = jnp.repeat(tokens, top_count, axis=0)
    outgoing = jnp.dot(dispatch_matrix, repeated, preferred_element_type=jnp.float32).astype(
        jnp.bfloat16
    )
    outgoing = outgoing.reshape(expert_count, capacity, feat_width)
    rank_partial = jnp.einsum(
        "scd,dr->scr",
        lax.all_to_all(outgoing, "exp", split_axis=0, concat_axis=0, tiled=True),
        adapter_in[0],
        preferred_element_type=jnp.float32,
    )
    rank_mid = lax.psum(rank_partial, "tp").astype(jnp.bfloat16)
    expert_out = jnp.einsum(
        "scr,rd->scd", rank_mid, adapter_out[0], preferred_element_type=jnp.float32
    ).astype(jnp.bfloat16)
    returned = lax.all_to_all(expert_out, "exp", split_axis=0, concat_axis=0, tiled=True)
    adapter_sum = jnp.dot(
        combine_matrix,
        returned.reshape(expert_count * capacity, feat_width).astype(jnp.float32),
        precision=lax.Precision.HIGHEST,
        preferred_element_type=jnp.float32,
    )
    return (base_out + adapter_sum).astype(jnp.bfloat16)


def solution(mesh):
    in_specs = (
        P(("grp", "exp"), "tp"),
        P("tp", None, "exp"),
        P("exp", "tp"),
        P("exp", "tp", None),
        P("exp", None, "tp"),
        P(("grp", "exp"), None),
        P(("grp", "exp"), None),
    )
    out_specs = P(("grp", "exp"), "tp")
    return jax.shard_map(local, mesh=mesh, in_specs=in_specs, out_specs=out_specs, check_vma=False)
```

profile of v0, /device:TPU:0, one launch (start us, length us, event | category | flops | bytes accessed | tf_op | source)
XLA Modules:
  0.0 105.8 jit_solution(269650311221717586)
XLA Ops:
  6.5 15.4 %all_gather.6 = bf16[64,896]{1,0:T(8,128)(2,1)S(1)} all-gather(bf16[16,896]{1,0:T(8,128)(2,1)} %param.7), channel_id=1, replica_groups=mesh['grp'=2,'exp'=4,'tp'=4] {'exp'}, dimensions={0}, use_global_device_ids=true | all-gather | bytes 143360 | tf_op jit(solution)/shard_map/all_gather | solution.py:10
  22.0 9.7 %copy.22 = bf16[112,8,2,4736]{3,1,2,0:T(8,128)(2,1)S(1)} copy(bf16[112,8,2,4736]{3,2,1,0:T(2,128)(2,1)} %bitcast.22) | data formatting | bytes 33947648
  31.7 3.5 %convolution_convert_fusion = bf16[64,9472]{1,0:T(8,128)(2,1)} fusion(bf16[64,896]{1,0:T(8,128)(2,1)S(1)} %all_gather.6, bf16[896,9472]{1,0:T(8,128)(2,1)S(1)} %bitcast.21), kind=kOutput, calls=%fused_computation | convolution fusion | flops 1086930944 | bytes 18300928 | tf_op jit(solution)/shard_map/dot_general | solution.py:14
  35.2 0.1 copy.20
  35.3 0.1 eq.35
  35.5 0.1 fusion.6
  35.5 0.1 reduce_window_sum.11
  35.6 0.2 select_reduce_fusion.1
  35.8 1.0 convolution_convert_fusion.2
  36.8 4.8 %all-to-all-start = ((bf16[4,16,896]{2,1,0:T(8,128)(2,1)}), bf16[4,16,896]{2,1,0:T(8,128)(2,1)S(1)}, u32[]{:S(2)}, u32[]{:S(2)}) async-start(bf16[4,16,896]{2,1,0:T(8,128)(2,1)} %bitcast), calls=%async_computation.2 | async-start | bytes 229376 | tf_op jit(solution)/shard_map/all_to_all | solution.py:56
  41.6 0.1 reduce_sum.21
  41.6 0.1 copy.21
  41.7 5.7 %all-to-all-done = bf16[4,16,896]{2,1,0:T(8,128)(2,1)S(1)} async-done(((bf16[4,16,896]{2,1,0:T(8,128)(2,1)}), bf16[4,16,896]{2,1,0:T(8,128)(2,1)S(1)}, u32[]{:S(2)}, u32[]{:S(2)}) %all-to-all-start) | async-done | bytes 114720 | tf_op jit(solution)/shard_map/all_to_all | solution.py:56
  47.4 0.2 fusion.3
  47.6 11.2 %psum.7 = bf16[4,16,16]{2,1,0:T(8,128)(2,1)S(1)} all-reduce(f32[4,16,16]{2,1,0:T(8,128)S(1)} %fusion.3), channel_id=1, replica_groups=mesh['grp'=2,'exp'=4,'tp'=4] {'tp'}, use_global_device_ids=true, to_apply=%region_5.6 | all-reduce | flops 1024 | bytes 6144 | tf_op jit(solution)/shard_map/psum | solution.py:60
  58.8 0.8 convolution_convert_fusion.1
  59.6 3.3 %all-to-all-start.1 = ((bf16[4,16,896]{2,1,0:T(8,128)(2,1)}), bf16[4,16,896]{2,1,0:T(8,128)(2,1)S(1)}, u32[]{:S(2)}, u32[]{:S(2)}) async-start(bf16[4,16,896]{2,1,0:T(8,128)(2,1)} %convolution_convert_fusion.1), calls=%async_computation.3 | async-start | bytes 229376 | tf_op jit(solution)/shard_map/all_to_all | solution.py:64
  63.0 1.0 convert_element_type.34
  64.0 0.1 fusion.1
  64.1 7.7 %all_gather.7 = bf16[64,4736]{1,0:T(8,128)(2,1)S(1)} all-gather(bf16[16,4736]{1,0:T(8,128)(2,1)S(1)} %fusion.1), channel_id=1, replica_groups=mesh['grp'=2,'exp'=4,'tp'=4] {'tp'}, dimensions={0}, use_global_device_ids=true | all-gather | bytes 757760 | tf_op jit(solution)/shard_map/all_gather | solution.py:22
  71.8 5.5 %convolution_convert_fusion.3 = bf16[64,896]{1,0:T(8,128)(2,1)} fusion(bf16[64,4736]{1,0:T(8,128)(2,1)S(1)} %all_gather.7, bf16[4736,896]{1,0:T(8,128)(2,1)} %param.9), kind=kOutput, calls=%fused_computation.3 | convolution fusion | flops 543219712 | bytes 9207808 | tf_op jit(solution)/shard_map/dot_general | solution.py:24
  77.3 0.1 select_reduce_fusion
  77.4 20.0 %reduce-scatter.5.cloned.1.call-done = bf16[16,896]{1,0:T(8,128)(2,1)} async-done(((bf16[64,896]{1,0:T(8,128)(2,1)}), bf16[16,896]{1,0:T(8,128)(2,1)}) %reduce-scatter.5.cloned.1.call-update) | async-done | bytes 28688 | tf_op jit(solution)/shard_map/reduce_scatter | solution.py:23
  97.4 1.5 %fusion = bf16[16,896]{1,0:T(8,128)(2,1)} fusion(f32[16,64]{1,0:T(8,128)S(1)} %select_reduce_fusion, bf16[64,896]{1,0:T(8,128)(2,1)S(1)} %bitcast.23, bf16[16,896]{1,0:T(8,128)(2,1)} %reduce-scatter.5.cloned.1.call-done), kind=kOutput, calls=%fused_computation.5 | convolution fusion | flops 11053056 | bytes 176128 | tf_op jit(solution)/shard_map/dot_general | solution.py:65
  (20 shorter events, 0.2 us)
Async XLA Ops:
  6.5 52.3 %copy-start = (bf16[1,16,896]{2,1,0:T(8,128)(2,1)S(1)}, bf16[1,16,896]{2,1,0:T(8,128)(2,1)}, u32[]{:S(2)}) copy-start(bf16[1,16,896]{2,1,0:T(8,128)(2,1)} %param.11) | copy-start | bytes 86020
  6.5 56.4 %reduce-scatter.3.cloned.1.call-start = ((), (), s32[]{:S(2)}) async-start(), calls=%async_computation.4 | async-start | bytes 1515520 | tf_op jit(solution)/shard_map/reduce_scatter | solution.py:13
  31.7 3.5 %copy-start.3 = (s32[16,2]{0,1:T(2,128)S(1)}, s32[16,2]{0,1:T(2,128)}, u32[]{:S(2)}) copy-start(s32[16,2]{0,1:T(2,128)} %param.12) | copy-start | bytes 388
  31.7 3.7 %copy-start.1 = (bf16[16,896]{1,0:T(8,128)(2,1)S(1)}, bf16[16,896]{1,0:T(8,128)(2,1)}, u32[]{:S(2)}) copy-start(bf16[16,896]{1,0:T(8,128)(2,1)} %param.7) | copy-start | bytes 86020
  31.7 15.7 %copy-start.2 = (bf16[1,896,16]{1,2,0:T(8,128)(2,1)S(1)}, bf16[1,896,16]{1,2,0:T(8,128)(2,1)}, u32[]{:S(2)}) copy-start(bf16[1,896,16]{1,2,0:T(8,128)(2,1)} %param.10) | copy-start | bytes 86020
  36.8 10.7 %all-to-all-start = ((bf16[4,16,896]{2,1,0:T(8,128)(2,1)}), bf16[4,16,896]{2,1,0:T(8,128)(2,1)S(1)}, u32[]{:S(2)}, u32[]{:S(2)}) async-start(bf16[4,16,896]{2,1,0:T(8,128)(2,1)} %bitcast), calls=%async_computation.2 | async-start | bytes 229376 | tf_op jit(solution)/shard_map/all_to_all | solution.py:56
  59.6 17.8 %all-to-all-start.1 = ((bf16[4,16,896]{2,1,0:T(8,128)(2,1)}), bf16[4,16,896]{2,1,0:T(8,128)(2,1)S(1)}, u32[]{:S(2)}, u32[]{:S(2)}) async-start(bf16[4,16,896]{2,1,0:T(8,128)(2,1)} %convolution_convert_fusion.1), calls=%async_computation.3 | async-start | bytes 229376 | tf_op jit(solution)/shard_map/all_to_all | solution.py:64
  62.9 34.5 %reduce-scatter.5.cloned.1.call-start = ((), (), s32[]{:S(2)}) async-start(), calls=%async_computation.5 | async-start | bytes 143360 | tf_op jit(solution)/shard_map/reduce_scatter | solution.py:23
  71.8 5.5 %copy-start.4 = (f32[16,2]{0,1:T(2,128)S(1)}, f32[16,2]{0,1:T(2,128)}, u32[]{:S(2)}) copy-start(f32[16,2]{0,1:T(2,128)} %param.13) | copy-start | bytes 388
Sparse Core Ops, SparseCore 0:
  35.3 27.2 reduce-scatter.2
  77.4 19.9 reduce-scatter.4
where the time goes:
time: 106 us
  blocking collectives  34.4 us (32%)
  waiting for transfers between devices  25.7 us (24%)
  between operations  13.5 us (13%)
  matrix products  12.4 us (12%)
  local copies, waits for them, and re-layouts  10.1 us (10%)
  starting transfers between devices  8.16 us (8%)
  other arithmetic  1.49 us (1%)
    reduce_scatter x1, waiting for transfers between devices, local(): lax.psum_scatter(jnp.dot(hidden, down_weight, preferred_element_type=jnp....  20 us
    all_gather x1, blocking collectives, local(): all_tokens = lax.all_gather(tokens, 'exp', axis=0, tiled=True)  15.4 us
    psum x1, blocking collectives, local(): rank_mid = lax.psum(rank_partial, 'tp').astype(jnp.bfloat16)  11.2 us
    unnamed x12, local copies, waits for them, and re-layouts  9.81 us
    all_gather x1, blocking collectives, local(): hidden = lax.all_gather(hidden_share, 'tp', axis=0, tiled=True)  7.73 us
    all_to_all x1, waiting for transfers between devices, local(): lax.all_to_all(outgoing, 'exp', split_axis=0, concat_axis=0, tiled=True)  5.71 us
    dot_general x1, matrix products, local(): jnp.dot(hidden, down_weight, preferred_element_type=jnp.float32)  5.47 us
    all_to_all x1, starting transfers between devices, local(): lax.all_to_all(outgoing, 'exp', split_axis=0, concat_axis=0, tiled=True)  4.8 us
  transfers between devices with their start and end apart: 4, of which 2 were waited for; matrix products, arithmetic and copies ran while one was open for 9% of the time, Pallas kernels for 0%

commit v1 on v0

--- a/solution.py
+++ b/solution.py
@@ -57,7 +57,7 @@
         adapter_in[0],
         preferred_element_type=jnp.float32,
     )
-    rank_mid = lax.psum(rank_partial, "tp").astype(jnp.bfloat16)
+    rank_mid = jnp.sum(lax.all_gather(rank_partial, "tp"), axis=0).astype(jnp.bfloat16)
     expert_out = jnp.einsum(
         "scr,rd->scd", rank_mid, adapter_out[0], preferred_element_type=jnp.float32
     ).astype(jnp.bfloat16)

time: 106 us -> 105 us (level)
  blocking collectives: 34.4 us -> 27.9 us
  waiting for transfers between devices: 25.7 us -> 31 us
    psum x1 -> x0, blocking collectives: 11.2 us -> none  [local(): rank_mid = lax.psum(rank_partial, 'tp').astype(jnp.bfloat16)]
    all_gather x0 -> x1, blocking collectives: none -> 5.42 us  [local(): lax.all_gather(rank_partial, 'tp')]
    reduce_scatter x1, waiting for transfers between devices: 0.02 us -> 5.19 us  [local(): lax.psum_scatter(jnp.dot(all_tokens, pair_weight, preferred_element_type=...]
  transfers between devices with their start and end apart: 4 -> 4, of which waited for: 2 -> 3; matrix products, arithmetic and copies ran while one was open for 9% -> 9% of each run, Pallas kernels for 0% -> 0%
where the time goes in v1:
time: 105 us
  waiting for transfers between devices  31 us (30%)
  blocking collectives  27.9 us (27%)
  between operations  13.5 us (13%)
  matrix products  12.4 us (12%)
  local copies, waits for them, and re-layouts  10.1 us (10%)
  starting transfers between devices  8.16 us (8%)
  other arithmetic  1.51 us (1%)
    reduce_scatter x1, waiting for transfers between devices, local(): lax.psum_scatter(jnp.dot(hidden, down_weight, preferred_element_type=jnp....  20 us
    all_gather x1, blocking collectives, local(): all_tokens = lax.all_gather(tokens, 'exp', axis=0, tiled=True)  15.4 us
    unnamed x12, local copies, waits for them, and re-layouts  9.81 us
    all_gather x1, blocking collectives, local(): hidden = lax.all_gather(hidden_share, 'tp', axis=0, tiled=True)  7.04 us
    all_to_all x1, waiting for transfers between devices, local(): lax.all_to_all(outgoing, 'exp', split_axis=0, concat_axis=0, tiled=True)  5.71 us
    dot_general x1, matrix products, local(): jnp.dot(hidden, down_weight, preferred_element_type=jnp.float32)  5.46 us
    all_gather x1, blocking collectives, local(): lax.all_gather(rank_partial, 'tp')  5.42 us
    reduce_scatter x1, waiting for transfers between devices, local(): lax.psum_scatter(jnp.dot(all_tokens, pair_weight, preferred_element_type=...  5.19 us
  transfers between devices with their start and end apart: 4, of which 3 were waited for; matrix products, arithmetic and copies ran while one was open for 9% of the time, Pallas kernels for 0%

profile of v1, /device:TPU:0, one launch (start us, length us, event | category | flops | bytes accessed | tf_op | source)
XLA Modules:
  0.0 104.5 jit_solution(14898736742309367165)
XLA Ops:
  6.5 15.4 %all_gather.12 = bf16[64,896]{1,0:T(8,128)(2,1)S(1)} all-gather(bf16[16,896]{1,0:T(8,128)(2,1)} %param.7), channel_id=1, replica_groups=mesh['grp'=2,'exp'=4,'tp'=4] {'exp'}, dimensions={0}, use_global_device_ids=true | all-gather | bytes 143360 | tf_op jit(solution)/shard_map/all_gather | solution.py:10
  22.0 9.7 %copy.26 = bf16[112,8,2,4736]{3,1,2,0:T(8,128)(2,1)S(1)} copy(bf16[112,8,2,4736]{3,2,1,0:T(2,128)(2,1)} %bitcast.23) | data formatting | bytes 33947648
  31.7 3.5 %convolution_convert_fusion = bf16[64,9472]{1,0:T(8,128)(2,1)} fusion(bf16[64,896]{1,0:T(8,128)(2,1)S(1)} %all_gather.12, bf16[896,9472]{1,0:T(8,128)(2,1)S(1)} %bitcast.22), kind=kOutput, calls=%fused_computation | convolution fusion | flops 1086930944 | bytes 18300928 | tf_op jit(solution)/shard_map/dot_general | solution.py:14
  35.2 0.1 copy.24
  35.3 0.1 eq.35
  35.5 0.1 fusion.6
  35.6 0.2 select_reduce_fusion.1
  35.8 1.0 convolution_convert_fusion.2
  36.8 4.8 %all-to-all-start = ((bf16[4,16,896]{2,1,0:T(8,128)(2,1)}), bf16[4,16,896]{2,1,0:T(8,128)(2,1)S(1)}, u32[]{:S(2)}, u32[]{:S(2)}) async-start(bf16[4,16,896]{2,1,0:T(8,128)(2,1)} %bitcast), calls=%async_computation.2 | async-start | bytes 229376 | tf_op jit(solution)/shard_map/all_to_all | solution.py:56
  41.6 0.1 reduce_sum.30
  41.6 0.1 copy.25
  41.7 5.7 %all-to-all-done = bf16[4,16,896]{2,1,0:T(8,128)(2,1)S(1)} async-done(((bf16[4,16,896]{2,1,0:T(8,128)(2,1)}), bf16[4,16,896]{2,1,0:T(8,128)(2,1)S(1)}, u32[]{:S(2)}, u32[]{:S(2)}) %all-to-all-start) | async-done | bytes 114720 | tf_op jit(solution)/shard_map/all_to_all | solution.py:56
  47.4 0.2 fusion.3
  47.6 5.4 %all-gather = f32[16,16,16]{2,1,0:T(8,128)S(1)} all-gather(f32[4,16,16]{2,1,0:T(8,128)S(1)} %fusion.3), channel_id=2, replica_groups=mesh['grp'=2,'exp'=4,'tp'=4] {'tp'}, dimensions={0}, use_global_device_ids=true | all-gather | bytes 20480 | tf_op jit(solution)/shard_map/all_gather | solution.py:60
  53.0 0.8 convolution_convert_fusion.1
  53.8 3.3 %all-to-all-start.1 = ((bf16[4,16,896]{2,1,0:T(8,128)(2,1)}), bf16[4,16,896]{2,1,0:T(8,128)(2,1)S(1)}, u32[]{:S(2)}, u32[]{:S(2)}) async-start(bf16[4,16,896]{2,1,0:T(8,128)(2,1)} %convolution_convert_fusion.1), calls=%async_computation.3 | async-start | bytes 229376 | tf_op jit(solution)/shard_map/all_to_all | solution.py:64
  57.2 5.2 %reduce-scatter.3.cloned.1.call-done = bf16[16,9472]{1,0:T(8,128)(2,1)} async-done(((bf16[64,9472]{1,0:T(8,128)(2,1)}), bf16[16,9472]{1,0:T(8,128)(2,1)}) %reduce-scatter.3.cloned.1.call-update) | async-done | bytes 303120 | tf_op jit(solution)/shard_map/reduce_scatter | solution.py:13
  62.4 1.0 convert_element_type.34
  63.4 0.1 fusion.1
  63.5 7.0 %all_gather.13 = bf16[64,4736]{1,0:T(8,128)(2,1)S(1)} all-gather(bf16[16,4736]{1,0:T(8,128)(2,1)S(1)} %fusion.1), channel_id=1, replica_groups=mesh['grp'=2,'exp'=4,'tp'=4] {'tp'}, dimensions={0}, use_global_device_ids=true | all-gather | bytes 757760 | tf_op jit(solution)/shard_map/all_gather | solution.py:22
  70.6 5.5 %convolution_convert_fusion.3 = bf16[64,896]{1,0:T(8,128)(2,1)} fusion(bf16[64,4736]{1,0:T(8,128)(2,1)S(1)} %all_gather.13, bf16[4736,896]{1,0:T(8,128)(2,1)} %param.9), kind=kOutput, calls=%fused_computation.3 | convolution fusion | flops 543219712 | bytes 9207808 | tf_op jit(solution)/shard_map/dot_general | solution.py:24
  76.1 0.1 select_reduce_fusion
  76.2 20.0 %reduce-scatter.5.cloned.1.call-done = bf16[16,896]{1,0:T(8,128)(2,1)} async-done(((bf16[64,896]{1,0:T(8,128)(2,1)}), bf16[16,896]{1,0:T(8,128)(2,1)}) %reduce-scatter.5.cloned.1.call-update) | async-done | bytes 28688 | tf_op jit(solution)/shard_map/reduce_scatter | solution.py:23
  96.2 1.5 %fusion = bf16[16,896]{1,0:T(8,128)(2,1)} fusion(f32[16,64]{1,0:T(8,128)S(1)} %select_reduce_fusion, bf16[64,896]{1,0:T(8,128)(2,1)S(1)} %bitcast.25, bf16[16,896]{1,0:T(8,128)(2,1)} %reduce-scatter.5.cloned.1.call-done), kind=kOutput, calls=%fused_computation.5 | convolution fusion | flops 11053056 | bytes 176128 | tf_op jit(solution)/shard_map/dot_general | solution.py:65
  (21 shorter events, 0.2 us)
Async XLA Ops:
  6.5 46.5 %copy-start = (bf16[1,16,896]{2,1,0:T(8,128)(2,1)S(1)}, bf16[1,16,896]{2,1,0:T(8,128)(2,1)}, u32[]{:S(2)}) copy-start(bf16[1,16,896]{2,1,0:T(8,128)(2,1)} %param.11) | copy-start | bytes 86020
  6.5 55.9 %reduce-scatter.3.cloned.1.call-start = ((), (), s32[]{:S(2)}) async-start(), calls=%async_computation.4 | async-start | bytes 1515520 | tf_op jit(solution)/shard_map/reduce_scatter | solution.py:13
  31.7 3.5 %copy-start.3 = (s32[16,2]{0,1:T(2,128)S(1)}, s32[16,2]{0,1:T(2,128)}, u32[]{:S(2)}) copy-start(s32[16,2]{0,1:T(2,128)} %param.12) | copy-start | bytes 388
  31.7 3.7 %copy-start.1 = (bf16[16,896]{1,0:T(8,128)(2,1)S(1)}, bf16[16,896]{1,0:T(8,128)(2,1)}, u32[]{:S(2)}) copy-start(bf16[16,896]{1,0:T(8,128)(2,1)} %param.7) | copy-start | bytes 86020
  31.7 15.7 %copy-start.2 = (bf16[1,896,16]{1,2,0:T(8,128)(2,1)S(1)}, bf16[1,896,16]{1,2,0:T(8,128)(2,1)}, u32[]{:S(2)}) copy-start(bf16[1,896,16]{1,2,0:T(8,128)(2,1)} %param.10) | copy-start | bytes 86020
  36.8 10.7 %all-to-all-start = ((bf16[4,16,896]{2,1,0:T(8,128)(2,1)}), bf16[4,16,896]{2,1,0:T(8,128)(2,1)S(1)}, u32[]{:S(2)}, u32[]{:S(2)}) async-start(bf16[4,16,896]{2,1,0:T(8,128)(2,1)} %bitcast), calls=%async_computation.2 | async-start | bytes 229376 | tf_op jit(solution)/shard_map/all_to_all | solution.py:56
  53.8 22.3 %all-to-all-start.1 = ((bf16[4,16,896]{2,1,0:T(8,128)(2,1)}), bf16[4,16,896]{2,1,0:T(8,128)(2,1)S(1)}, u32[]{:S(2)}, u32[]{:S(2)}) async-start(bf16[4,16,896]{2,1,0:T(8,128)(2,1)} %convolution_convert_fusion.1), calls=%async_computation.3 | async-start | bytes 229376 | tf_op jit(solution)/shard_map/all_to_all | solution.py:64
  57.2 39.0 %reduce-scatter.5.cloned.1.call-start = ((), (), s32[]{:S(2)}) async-start(), calls=%async_computation.5 | async-start | bytes 143360 | tf_op jit(solution)/shard_map/reduce_scatter | solution.py:23
  70.6 5.5 %copy-start.4 = (f32[16,2]{0,1:T(2,128)S(1)}, f32[16,2]{0,1:T(2,128)}, u32[]{:S(2)}) copy-start(f32[16,2]{0,1:T(2,128)} %param.13) | copy-start | bytes 388
Sparse Core Ops, SparseCore 0:
  35.3 27.0 reduce-scatter.2
  76.2 19.9 reduce-scatter.4
